TPU v7x, 32 devices: a whole 2x2x4 slice. The times are simulated.
32 devices in a mesh: row: 4 (over y, core), col: 8 (over z, x).
Axes of the slice: x: 2, y: 2, z: 4, core: 2. Of those that a mesh axis runs over, the one named last changes fastest.
Arguments:
- matrix: float32 [4096, 4096], P('row', 'col'), may hold values from -12 to 12, as said below
Outputs:
- sign_estimate: float32 [4096, 4096], P('row', 'col')
Inputs may be any that keep to these rules, and one draw needn't show every extreme that they name: `matrix`: symmetric; the magnitudes of its eigenvalues, divided by the root mean square of all its eigenvalues, lie between 0.4 and 1.7.
All inputs are finite; a program needn't handle non-finite values.
Results may differ from a plain program's by a relative error of at most 0.0002.
Values sent between devices are 32-bit elements; how exact they have to be, the bound alone decides.
A program may use at most 64 MiB of HBM per device.

v0:
```python
import jax
import jax.numpy as jnp
from jax import lax
from jax.sharding import PartitionSpec as P

N = 4096
ITERS = 2


def shards(matrix):
    total = lax.psum(jnp.sum(matrix * matrix), ("row", "col"))
    factor = jnp.sqrt(N / total)
    x_iter = matrix * factor
    for step in range(ITERS):
        source = x_iter
        rows_panel = lax.all_gather(source, "col", axis=1, tiled=True)
        cols_panel = lax.all_gather(source, "row", axis=0, tiled=True)
        square = jnp.dot(
            rows_panel,
            cols_panel,
            preferred_element_type=jnp.float32,
            precision=lax.Precision.HIGHEST,
        )
        cube_block = jnp.dot(
            rows_panel,
            lax.all_gather(square, "row", axis=0, tiled=True),
            preferred_element_type=jnp.float32,
            precision=lax.Precision.HIGHEST,
        )
        x_iter = 1.5 * x_iter - 0.5 * cube_block
    return x_iter


def solution(mesh):
    in_specs = (P("row", "col"),)
    out_specs = P("row", "col")
    return jax.shard_map(shards, mesh=mesh, in_specs=in_specs, out_specs=out_specs, check_vma=False)
```

profile of v0, /device:TPU:0, one launch (start us, length us, event | category | flops | bytes accessed | tf_op | source)
XLA Modules:
  0.0 875.6 jit_solution(11313682879477920894)
XLA Ops:
  6.5 2.7 multiply_reduce_fusion
  9.3 42.2 %psum.7 = f32[]{:T(128)} all-reduce(f32[]{:T(128)} %multiply_reduce_fusion), channel_id=1, replica_groups=mesh['row'=4,'col'=8] {'row','col'}, use_global_device_ids=true, to_apply=%region_1.0 | all-reduce | flops 1 | bytes 8 | tf_op jit(solution)/shard_map/psum | solution.py:11
  52.2 3.1 broadcast_multiply_fusion
  55.3 0.0 all-gather.9.cloned.1.call-update
  55.3 0.0 all-gather.7.cloned.1.call-start
  55.4 0.7 all-gather.7.cloned.1.call-update
  56.1 0.0 all-gather.11.cloned.1.call-start
  56.1 57.6 %all-gather.9.cloned.1.call-done = f32[4096,512]{1,0:T(8,128)} async-done(((f32[1024,512]{1,0:T(8,128)}), f32[4096,512]{1,0:T(8,128)}) %all-gather.9.cloned.1.call-update) | async-done | bytes 8388624 | tf_op jit(solution)/shard_map/all_gather | solution.py:17
  113.7 229.5 %all-gather.7.cloned.1.call-done = f32[1024,4096]{1,0:T(8,128)} async-done(((f32[1024,512]{1,0:T(8,128)}), f32[1024,4096]{1,0:T(8,128)}) %all-gather.7.cloned.1.call-update) | async-done | bytes 16777232 | tf_op jit(solution)/shard_map/all_gather | solution.py:16
  343.2 31.0 %fusion = f32[1024,512]{1,0:T(8,128)} fusion(f32[1024,4096]{1,0:T(8,128)} %all-gather.7.cloned.1.call-done, f32[4096,512]{1,0:T(8,128)} %all-gather.9.cloned.1.call-done), kind=kOutput, calls=%fused_computation.4 | convolution fusion | flops 25769803776 | bytes 27262976 | tf_op jit(solution)/shard_map/dot_general | solution.py:18
  374.2 0.0 all-gather.11.cloned.1.call-update
  374.2 0.2 all-gather.15.cloned.1.call-start
  374.5 56.4 %all-gather.11.cloned.1.call-done = f32[4096,512]{1,0:T(8,128)} async-done(((f32[1024,512]{1,0:T(8,128)}), f32[4096,512]{1,0:T(8,128)}) %all-gather.11.cloned.1.call-update) | async-done | bytes 8388624 | tf_op jit(solution)/shard_map/all_gather | solution.py:26
  430.8 31.2 %multiply_subtract_fusion.1 = f32[1024,512]{1,0:T(8,128)} fusion(f32[1024,512]{1,0:T(8,128)S(1)} %copy-done, f32[1024,4096]{1,0:T(8,128)} %all-gather.7.cloned.1.call-done, f32[4096,512]{1,0:T(8,128)} %all-gather.11.cloned.1.call-done), kind=kOutput, calls=%fused_computation.1 | convolution fusion | flops 25771376640 | bytes 29360128 | tf_op jit(solution)/shard_map/dot_general | solution.py:24
  462.1 0.0 all-gather.15.cloned.1.call-update
  462.1 0.0 all-gather.13.cloned.1.call-start
  462.1 0.5 all-gather.13.cloned.1.call-update
  462.7 0.3 all-gather.17.cloned.1.call-start
  463.0 57.6 %all-gather.15.cloned.1.call-done = f32[4096,512]{1,0:T(8,128)} async-done(((f32[1024,512]{1,0:T(8,128)}), f32[4096,512]{1,0:T(8,128)}) %all-gather.15.cloned.1.call-update) | async-done | bytes 8388624 | tf_op jit(solution)/shard_map/all_gather | solution.py:17
  520.5 229.3 %all-gather.13.cloned.1.call-done = f32[1024,4096]{1,0:T(8,128)} async-done(((f32[1024,512]{1,0:T(8,128)}), f32[1024,4096]{1,0:T(8,128)}) %all-gather.13.cloned.1.call-update) | async-done | bytes 16777232 | tf_op jit(solution)/shard_map/all_gather | solution.py:16
  749.8 31.0 %fusion.1 = f32[1024,512]{1,0:T(8,128)} fusion(f32[1024,4096]{1,0:T(8,128)} %all-gather.13.cloned.1.call-done, f32[4096,512]{1,0:T(8,128)} %all-gather.15.cloned.1.call-done), kind=kOutput, calls=%fused_computation.5 | convolution fusion | flops 25769803776 | bytes 27262976 | tf_op jit(solution)/shard_map/dot_general | solution.py:18
  780.9 0.0 all-gather.17.cloned.1.call-update
  780.9 56.6 %all-gather.17.cloned.1.call-done = f32[4096,512]{1,0:T(8,128)} async-done(((f32[1024,512]{1,0:T(8,128)}), f32[4096,512]{1,0:T(8,128)}) %all-gather.17.cloned.1.call-update) | async-done | bytes 8388624 | tf_op jit(solution)/shard_map/all_gather | solution.py:26
  837.5 31.2 %multiply_subtract_fusion = f32[1024,512]{1,0:T(8,128)} fusion(f32[1024,512]{1,0:T(8,128)S(1)} %copy-done.1, f32[1024,4096]{1,0:T(8,128)} %all-gather.13.cloned.1.call-done, f32[4096,512]{1,0:T(8,128)} %all-gather.17.cloned.1.call-done), kind=kOutput, calls=%fused_computation | convolution fusion | flops 25771376640 | bytes 29360128 | tf_op jit(solution)/shard_map/dot_general | solution.py:24
  (5 shorter events, 0.0 us)
Async XLA Ops:
  6.5 107.2 %all-gather.9.cloned.1.call-start = ((), (), s32[]{:S(2)}) async-start(), calls=%async_computation.1 | async-start | bytes 10485760 | tf_op jit(solution)/shard_map/all_gather | solution.py:17
  55.3 287.9 %all-gather.7.cloned.1.call-start = ((), (), s32[]{:S(2)}) async-start(), calls=%async_computation | async-start | bytes 18874368 | tf_op jit(solution)/shard_map/all_gather | solution.py:16
  56.1 374.8 %copy-start = (f32[1024,512]{1,0:T(8,128)S(1)}, f32[1024,512]{1,0:T(8,128)}, u32[]{:S(2)}) copy-start(f32[1024,512]{1,0:T(8,128)} %broadcast_multiply_fusion) | copy-start | bytes 6291460
  56.1 374.8 %all-gather.11.cloned.1.call-start = ((), (), s32[]{:S(2)}) async-start(), calls=%async_computation.2 | async-start | bytes 10485760 | tf_op jit(solution)/shard_map/all_gather | solution.py:26
  374.2 146.3 %all-gather.15.cloned.1.call-start = ((), (), s32[]{:S(2)}) async-start(), calls=%async_computation.4 | async-start | bytes 10485760 | tf_op jit(solution)/shard_map/all_gather | solution.py:17
  462.1 287.7 %all-gather.13.cloned.1.call-start = ((), (), s32[]{:S(2)}) async-start(), calls=%async_computation.3 | async-start | bytes 18874368 | tf_op jit(solution)/shard_map/all_gather | solution.py:16
  462.7 374.8 %copy-start.1 = (f32[1024,512]{1,0:T(8,128)S(1)}, f32[1024,512]{1,0:T(8,128)}, u32[]{:S(2)}) copy-start(f32[1024,512]{1,0:T(8,128)} %multiply_subtract_fusion.1) | copy-start | bytes 6291460
  462.7 374.8 %all-gather.17.cloned.1.call-start = ((), (), s32[]{:S(2)}) async-start(), calls=%async_computation.5 | async-start | bytes 10485760 | tf_op jit(solution)/shard_map/all_gather | solution.py:26
Sparse Core Ops, SparseCore 0:
  55.4 58.2 all-gather.8
  115.9 227.2 all-gather.6
  374.4 56.4 all-gather.10
  462.2 58.2 all-gather.14
  522.6 227.2 all-gather.12
  781.0 56.4 all-gather.16
where the time goes:
time: 876 us
  waiting for transfers between devices  688 us (79%)
  matrix products  125 us (14%)
  blocking collectives  42.2 us (5%)
  between operations  14.2 us (2%)
    all_gather x2, waiting for transfers between devices, shards(): rows_panel = lax.all_gather(source, 'col', axis=1, tiled=True)  459 us
    all_gather x2, waiting for transfers between devices, shards(): cols_panel = lax.all_gather(source, 'row', axis=0, tiled=True)  115 us
    all_gather x2, waiting for transfers between devices, shards(): lax.all_gather(square, 'row', axis=0, tiled=True)  113 us
    dot_general x2, matrix products, shards(): jnp.dot(rows_panel, lax.all_gather(square, 'row', axis=0, tiled=True), pr...  62.5 us
    dot_general x2, matrix products, shards(): jnp.dot(rows_panel, cols_panel, preferred_element_type=jnp.float32, preci...  62 us
    psum x1, blocking collectives, shards(): total = lax.psum(jnp.sum(matrix * matrix), ('row', 'col'))  42.2 us
  transfers between devices with their start and end apart: 6, of which 6 were waited for; matrix products, arithmetic and copies ran while one was open for 0% of the time, Pallas kernels for 0%

commit v1 on v0

v1 whole, which is shorter than its diff:
```python
import functools

import jax
import jax.numpy as jnp
from jax import lax
from jax.experimental import pallas as pl
from jax.experimental.pallas import tpu as pltpu
from jax.sharding import PartitionSpec as P

ITERS = 2
PIECES = 4
MESH = pl.DeviceIdType.MESH


class Gather:
    def __init__(self, axis, size, src, slot, line, pair, sends, copy_sem):
        self.axis, self.src, self.slot = axis, src, slot
        self.line, self.pair, self.sends, self.copy_sem = line, pair, sends, copy_sem
        me = lax.axis_index(axis)
        self.spots = size // 2
        self.spot, self.side = me // 2, lax.rem(me, 2)
        self.partner = me + 1 - 2 * self.side
        self.left, self.right = me - 2, me + 2
        self.pieces = PIECES
        self.depth = src.shape[0] // PIECES

    def ends(self):
        return ((self.left, self.spot > 0), (self.right, self.spot < self.spots - 1))

    def greet(self, barrier):
        pl.semaphore_signal(barrier, inc=1, device_id={self.axis: self.partner}, device_id_type=MESH)
        for target, there in self.ends():
            @pl.when(there)
            def _():
                pl.semaphore_signal(barrier, inc=1, device_id={self.axis: target}, device_id_type=MESH)

    def peers(self):
        return 1 + sum(there.astype(jnp.int32) for _, there in self.ends())

    def part(self, ref, piece):
        return ref.at[pl.ds(piece * self.depth, self.depth), :]

    def copy(self, spot, piece, way, own):
        dst = self.part(self.slot(2 * spot + self.side), piece)
        src = self.part(self.src, piece) if own else dst
        sems = self.pair if way == 2 else self.line
        target = (self.left, self.right, self.partner)[way]
        return pltpu.make_async_remote_copy(
            src_ref=src, dst_ref=dst, send_sem=self.sends.at[way, spot, piece], recv_sem=sems.at[spot, piece],
            device_id={self.axis: target}, device_id_type=MESH)

    def arrive(self, spot, piece, side, sems):
        dst = self.part(self.slot(2 * spot + side), piece)
        pltpu.make_async_remote_copy(
            src_ref=dst, dst_ref=dst, send_sem=self.sends.at[2, spot, piece], recv_sem=sems.at[spot, piece],
            device_id={self.axis: self.partner}, device_id_type=MESH).wait_recv()

    def begin(self):
        self.keep = pltpu.make_async_copy(self.src, self.slot(2 * self.spot + self.side), self.copy_sem)
        self.keep.start()
        for piece in range(self.pieces):
            for way, (_, there) in enumerate(self.ends()):
                @pl.when(there)
                def _():
                    self.copy(self.spot, piece, way, True).start()
            self.copy(self.spot, piece, 2, True).start()

    def relay(self, far, piece):
        for way, spot in ((0, self.spot + far), (1, self.spot - far)):
            here = spot < self.spots if way == 0 else spot >= 0
            @pl.when(here)
            def _():
                self.arrive(spot, piece, self.side, self.line)
                @pl.when(self.ends()[way][1])
                def _():
                    self.copy(spot, piece, way, False).start()
                self.copy(spot, piece, 2, False).start()

    def finish(self):
        self.keep.wait()
        for far in range(self.spots):
            for piece in range(self.pieces):
                if far == 0:
                    self.arrive(self.spot, piece, 1 - self.side, self.pair)
                    for way, (_, there) in enumerate(self.ends()):
                        @pl.when(there)
                        def _():
                            self.copy(self.spot, piece, way, True).wait_send()
                    self.copy(self.spot, piece, 2, True).wait_send()
                    continue
                for way, spot in ((0, self.spot + far), (1, self.spot - far)):
                    here = spot < self.spots if way == 0 else spot >= 0
                    @pl.when(here)
                    def _():
                        self.arrive(spot, piece, 1 - self.side, self.pair)
                        @pl.when(self.ends()[way][1])
                        def _():
                            self.copy(spot, piece, way, False).wait_send()
                        self.copy(spot, piece, 2, False).wait_send()


def run_gathers(gathers):
    barrier = pltpu.get_barrier_semaphore()
    for g in gathers:
        g.greet(barrier)
    pl.semaphore_wait(barrier, sum(g.peers() for g in gathers))
    for g in gathers:
        g.begin()
    for far in range(1, max(g.spots for g in gathers)):
        for piece in range(PIECES):
            for g in gathers:
                if far < g.spots:
                    g.relay(far, piece)
    for g in gathers:
        g.finish()


def both_kernel(row_n, col_n, x_ref, rows_ref, cols_ref, line_c, pair_c, sends_c, line_r, pair_r, sends_r, copies):
    depth, width = x_ref.shape
    rows_slot = lambda i: rows_ref.at[:, pl.ds(pl.multiple_of(i * width, width), width)]
    cols_slot = lambda i: cols_ref.at[pl.ds(pl.multiple_of(i * depth, depth), depth), :]
    run_gathers((
        Gather("row", row_n, x_ref, cols_slot, line_r, pair_r, sends_r, copies.at[1]),
        Gather("col", col_n, x_ref, rows_slot, line_c, pair_c, sends_c, copies.at[0]),
    ))


def cols_kernel(row_n, x_ref, cols_ref, line_r, pair_r, sends_r, copies):
    depth = x_ref.shape[0]
    cols_slot = lambda i: cols_ref.at[pl.ds(pl.multiple_of(i * depth, depth), depth), :]
    run_gathers((Gather("row", row_n, x_ref, cols_slot, line_r, pair_r, sends_r, copies.at[0]),))


def sems(size):
    dma = pltpu.SemaphoreType.DMA
    return [dma((size // 2, PIECES)), dma((size // 2, PIECES)), dma((3, size // 2, PIECES))]


ANY = pl.BlockSpec(memory_space=pl.ANY)


def gather_both(x, row_n, col_n):
    depth, width = x.shape
    return pl.pallas_call(
        functools.partial(both_kernel, row_n, col_n),
        out_shape=(jax.ShapeDtypeStruct((depth, width * col_n), x.dtype),
                   jax.ShapeDtypeStruct((depth * row_n, width), x.dtype)),
        in_specs=[ANY], out_specs=(ANY, ANY),
        scratch_shapes=sems(col_n) + sems(row_n) + [pltpu.SemaphoreType.DMA((2,))],
        compiler_params=pltpu.CompilerParams(collective_id=0, has_side_effects=True),
        name="gather_both",
    )(x)


def gather_cols(x, row_n):
    depth, width = x.shape
    return pl.pallas_call(
        functools.partial(cols_kernel, row_n),
        out_shape=jax.ShapeDtypeStruct((depth * row_n, width), x.dtype),
        in_specs=[ANY], out_specs=ANY,
        scratch_shapes=sems(row_n) + [pltpu.SemaphoreType.DMA((1,))],
        compiler_params=pltpu.CompilerParams(collective_id=1, has_side_effects=True),
        name="gather_cols",
    )(x)


def dot(a, b):
    return jnp.dot(a, b, preferred_element_type=jnp.float32, precision=lax.Precision.HIGH)


def shards(row_n, col_n, matrix):
    depth = matrix.shape[0]
    factor = jnp.sqrt(depth * row_n / lax.psum(jnp.sum(matrix * matrix), ("row", "col")))
    x_iter = matrix
    for step in range(ITERS):
        rows_panel, cols_panel = gather_both(x_iter, row_n, col_n)
        square = dot(rows_panel, cols_panel)
        cube = dot(rows_panel, gather_cols(square, row_n))
        if step == 0:
            x_iter = factor * (1.5 * x_iter - (0.5 * factor * factor) * cube)
        else:
            x_iter = 1.5 * x_iter - 0.5 * cube
    return x_iter


def solution(mesh):
    body = functools.partial(shards, mesh.shape["row"], mesh.shape["col"])
    return jax.shard_map(body, mesh=mesh, in_specs=(P("row", "col"),), out_specs=P("row", "col"), check_vma=False)
```

time: 876 us -> 625 us (0.71)
  waiting for transfers between devices: 688 us -> 0 us
  Pallas kernels: 0 us -> 501 us
  matrix products: 125 us -> 78.3 us
  between operations: 14.2 us -> 0.79 us
    all_gather x6 -> x0, waiting for transfers between devices: 687 us -> none  [the longest x2 459 us: shards(): rows_panel = lax.all_gather(source, 'col', axis=1, tiled=True)]
    pallas_call x0 -> x4, Pallas kernels: none -> 501 us  [the longest x2 369 us: gather_both(): pl.pallas_call(functools.partial(both_kernel, row_n, col_n), out_shape=(j...]
    dot_general x4, matrix products: 125 us -> 78.3 us  [dot(): jnp.dot(a, b, preferred_element_type=jnp.float32, precision=lax.Precision...]
  transfers between devices with their start and end apart: 6 -> 0, of which waited for: 6 -> 0; matrix products, arithmetic and copies ran while one was open for 0% -> 0% of each run, Pallas kernels for 0% -> 0%
where the time goes in v1:
time: 625 us
  Pallas kernels  501 us (80%)
  matrix products  78.3 us (13%)
  blocking collectives  42.2 us (7%)
    pallas_call x2, Pallas kernels, gather_both(): pl.pallas_call(functools.partial(both_kernel, row_n, col_n), out_shape=(j...  369 us
    pallas_call x2, Pallas kernels, gather_cols(): pl.pallas_call(functools.partial(cols_kernel, row_n), out_shape=jax.Shape...  132 us
    dot_general x4, matrix products, dot(): jnp.dot(a, b, preferred_element_type=jnp.float32, precision=lax.Precision...  78.3 us
    psum x1, blocking collectives, shards(): lax.psum(jnp.sum(matrix * matrix), ('row', 'col'))  42.2 us

profile of v1, /device:TPU:0, one launch (start us, length us, event | category | flops | bytes accessed | tf_op | source)
XLA Modules:
  0.0 625.0 jit_solution(548073721670145497)
XLA Ops:
  0.0 2.7 multiply_reduce_fusion
  2.7 42.2 %psum.7 = f32[]{:T(128)} all-reduce(f32[]{:T(128)} %multiply_reduce_fusion), channel_id=1, replica_groups=mesh['row'=4,'col'=8] {'row','col'}, use_global_device_ids=true, to_apply=%region_1.0 | all-reduce | flops 1 | bytes 8 | tf_op jit(solution)/shard_map/psum | solution.py:173
  45.6 184.9 %gather_both.2 = (f32[1024,4096]{1,0:T(8,128)}, f32[4096,512]{1,0:T(8,128)}) custom-call(f32[1024,512]{1,0:T(8,128)} %x_ref.1), custom_call_target="tpu_custom_call" | custom-call | tf_op jit(solution)/shard_map/gather_both/pallas_call | solution.py:144
  230.6 19.3 %fusion.1.x_ref = f32[1024,512]{1,0:T(8,128)} fusion(f32[1024,4096]{1,0:T(8,128)} %get-tuple-element.9, f32[4096,512]{1,0:T(8,128)} %get-tuple-element.10), kind=kOutput, calls=%fused_computation.4 | convolution fusion | flops 12884901888 | bytes 27262976 | tf_op jit(solution)/shard_map/dot_general | solution.py:168
  249.9 0.0 copy-start
  249.9 65.8 %gather_cols.2 = f32[4096,512]{1,0:T(8,128)} custom-call(f32[1024,512]{1,0:T(8,128)} %fusion.1.x_ref), custom_call_target="tpu_custom_call" | custom-call | tf_op jit(solution)/shard_map/gather_cols/pallas_call | solution.py:157
  315.6 0.0 copy-done
  315.6 20.1 %fusion.x_ref = f32[1024,512]{1,0:T(8,128)} fusion(f32[1024,512]{1,0:T(8,128)S(1)} %copy-done, f32[4096,512]{1,0:T(8,128)} %gather_cols.2, f32[1024,4096]{1,0:T(8,128)} %get-tuple-element.9, f32[]{:T(128)S(6)} %mul.40, f32[]{:T(128)S(6)} %sqrt.3), kind=kOutput, calls=%fused_computation.1 | convolution fusion | flops 12886999040 | bytes 29360136 | tf_op jit(solution)/shard_map/dot_general | solution.py:168
  335.7 184.1 %gather_both.3 = (f32[1024,4096]{1,0:T(8,128)}, f32[4096,512]{1,0:T(8,128)}) custom-call(f32[1024,512]{1,0:T(8,128)} %fusion.x_ref), custom_call_target="tpu_custom_call" | custom-call | tf_op jit(solution)/shard_map/gather_both/pallas_call | solution.py:144
  519.8 19.4 %fusion.2.x_ref = f32[1024,512]{1,0:T(8,128)} fusion(f32[1024,4096]{1,0:T(8,128)} %get-tuple-element.11, f32[4096,512]{1,0:T(8,128)} %get-tuple-element.12), kind=kOutput, calls=%fused_computation.5 | convolution fusion | flops 12884901888 | bytes 27262976 | tf_op jit(solution)/shard_map/dot_general | solution.py:168
  539.2 0.0 copy-start.1
  539.2 66.3 %gather_cols.3 = f32[4096,512]{1,0:T(8,128)} custom-call(f32[1024,512]{1,0:T(8,128)} %fusion.2.x_ref), custom_call_target="tpu_custom_call" | custom-call | tf_op jit(solution)/shard_map/gather_cols/pallas_call | solution.py:157
  605.5 0.0 copy-done.1
  605.5 19.6 %multiply_subtract_fusion = f32[1024,512]{1,0:T(8,128)} fusion(f32[1024,512]{1,0:T(8,128)S(1)} %copy-done.1, f32[1024,4096]{1,0:T(8,128)} %get-tuple-element.11, f32[4096,512]{1,0:T(8,128)} %gather_cols.3), kind=kOutput, calls=%fused_computation.2 | convolution fusion | flops 12886474752 | bytes 29360128 | tf_op jit(solution)/shard_map/dot_general | solution.py:168
Async XLA Ops:
  249.9 65.8 %copy-start = (f32[1024,512]{1,0:T(8,128)S(1)}, f32[1024,512]{1,0:T(8,128)}, u32[]{:S(2)}) copy-start(f32[1024,512]{1,0:T(8,128)} %x_ref.1) | copy-start | bytes 6291460
  539.2 66.3 %copy-start.1 = (f32[1024,512]{1,0:T(8,128)S(1)}, f32[1024,512]{1,0:T(8,128)}, u32[]{:S(2)}) copy-start(f32[1024,512]{1,0:T(8,128)} %fusion.x_ref) | copy-start | bytes 6291460

commit v2 on v1

v2 whole, which is shorter than its diff:
```python
import functools

import jax
import jax.numpy as jnp
from jax import lax
from jax.experimental import pallas as pl
from jax.experimental.pallas import tpu as pltpu
from jax.sharding import PartitionSpec as P

ITERS = 2
PIECES = 8
MESH = pl.DeviceIdType.MESH


class Gather:
    def __init__(self, axis, size, src, slot, line, pair, sends, copy_sem, swapped=0):
        self.axis, self.src, self.slot = axis, src, slot
        self.line, self.pair, self.sends, self.copy_sem = line, pair, sends, copy_sem
        me = lax.axis_index(axis)
        self.spots = size // 2
        self.spot, self.side = me // 2, lax.rem(me, 2)
        self.partner = me + 1 - 2 * self.side
        self.left, self.right = me - 2, me + 2
        self.pieces = line.shape[1]
        self.depth = src.shape[0] // self.pieces
        self.swapped = swapped

    def ends(self):
        return ((self.left, self.spot > 0), (self.right, self.spot < self.spots - 1))

    def greet(self, barrier):
        pl.semaphore_signal(barrier, inc=1, device_id={self.axis: self.partner}, device_id_type=MESH)
        for target, there in self.ends():
            @pl.when(there)
            def _():
                pl.semaphore_signal(barrier, inc=1, device_id={self.axis: target}, device_id_type=MESH)

    def peers(self):
        return 1 + sum(there.astype(jnp.int32) for _, there in self.ends())

    def part(self, ref, piece):
        return ref.at[pl.ds(piece * self.depth, self.depth), :]

    def copy(self, spot, piece, way, own, other=False):
        side = 1 - self.side if other else self.side
        dst = self.part(self.slot(2 * spot + side), piece)
        src = self.part(self.src, piece) if own else dst
        sems = self.pair if way == 2 or other else self.line
        target = (self.left, self.right, self.partner)[way]
        return pltpu.make_async_remote_copy(
            src_ref=src, dst_ref=dst, send_sem=self.sends.at[way + 3 * other, spot, piece],
            recv_sem=sems.at[spot, piece], device_id={self.axis: target}, device_id_type=MESH)

    def arrive(self, spot, piece, side, sems):
        dst = self.part(self.slot(2 * spot + side), piece)
        pltpu.make_async_remote_copy(
            src_ref=dst, dst_ref=dst, send_sem=self.sends.at[2, spot, piece], recv_sem=sems.at[spot, piece],
            device_id={self.axis: self.partner}, device_id_type=MESH).wait_recv()

    def onward(self, act, spot, piece, ways, own, other=False):
        for way in ways:
            @pl.when(self.ends()[way][1])
            def _():
                getattr(self.copy(spot, piece, way, own, other), act)()

    def far_spots(self, far):
        return ((0, self.spot + far, self.spot + far < self.spots), (1, self.spot - far, self.spot >= far))

    def begin(self):
        self.keep = pltpu.make_async_copy(self.src, self.slot(2 * self.spot + self.side), self.copy_sem)
        self.keep.start()
        for piece in range(self.pieces):
            self.copy(self.spot, piece, 2, True).start()
            self.onward("start", self.spot, piece, (0, 1), True)

    def cross(self):
        for piece in range(self.swapped):
            self.arrive(self.spot, piece, 1 - self.side, self.pair)
            self.onward("start", self.spot, piece, (0, 1), False, True)

    def relay(self, far, piece):
        for way, spot, here in self.far_spots(far):
            @pl.when(here)
            def _():
                self.arrive(spot, piece, self.side, self.line)
                self.onward("start", spot, piece, (way,), False)
                if piece >= self.swapped:
                    self.copy(spot, piece, 2, False).start()

    def relay_crossed(self, far):
        for piece in range(self.swapped):
            for way, spot, here in self.far_spots(far):
                @pl.when(here)
                def _():
                    self.arrive(spot, piece, 1 - self.side, self.pair)
                    self.onward("start", spot, piece, (way,), False, True)

    def finish(self):
        self.keep.wait()
        for piece in range(self.pieces):
            crossed = piece < self.swapped
            if not crossed:
                self.arrive(self.spot, piece, 1 - self.side, self.pair)
            self.copy(self.spot, piece, 2, True).wait_send()
            self.onward("wait_send", self.spot, piece, (0, 1), True)
            if crossed:
                self.onward("wait_send", self.spot, piece, (0, 1), False, True)
        for far in range(1, self.spots):
            for piece in range(self.pieces):
                crossed = piece < self.swapped
                for way, spot, here in self.far_spots(far):
                    @pl.when(here)
                    def _():
                        if not crossed:
                            self.arrive(spot, piece, 1 - self.side, self.pair)
                            self.copy(spot, piece, 2, False).wait_send()
                        self.onward("wait_send", spot, piece, (way,), False)
                        if crossed:
                            self.onward("wait_send", spot, piece, (way,), False, True)


def run_gathers(gathers):
    barrier = pltpu.get_barrier_semaphore()
    for g in gathers:
        g.greet(barrier)
    pl.semaphore_wait(barrier, sum(g.peers() for g in gathers))
    for g in gathers:
        g.begin()
    for g in gathers:
        g.cross()
    for far in range(1, max(g.spots for g in gathers)):
        for piece in range(PIECES):
            for g in gathers:
                if far < g.spots and piece < g.pieces:
                    g.relay(far, piece)
        for g in gathers:
            if far < g.spots:
                g.relay_crossed(far)
    for g in gathers:
        g.finish()


def down(ref, depth):
    return lambda i: ref.at[pl.ds(pl.multiple_of(i * depth, depth), depth), :]


def across(ref, width):
    return lambda i: ref.at[:, pl.ds(pl.multiple_of(i * width, width), width)]


def both_kernel(row_n, col_n, x_ref, s_ref, rows_ref, cols_ref, stats_ref, *sems):
    depth, width = x_ref.shape
    copies = sems[9]
    run_gathers((
        Gather("col", col_n, s_ref, down(stats_ref, 8), *sems[6:9], copies.at[2]),
        Gather("row", row_n, x_ref, down(cols_ref, depth), *sems[3:6], copies.at[1]),
        Gather("col", col_n, x_ref, across(rows_ref, width), *sems[0:3], copies.at[0], swapped=1),
    ))


def cols_kernel(row_n, x_ref, s_ref, cols_ref, stats_ref, *sems):
    depth = x_ref.shape[0]
    copies = sems[6]
    run_gathers((
        Gather("row", row_n, s_ref, down(stats_ref, 8), *sems[3:6], copies.at[1]),
        Gather("row", row_n, x_ref, down(cols_ref, depth), *sems[0:3], copies.at[0]),
    ))


def sems(size, pieces):
    dma = pltpu.SemaphoreType.DMA
    return [dma((size // 2, pieces)), dma((size // 2, pieces)), dma((5, size // 2, pieces))]


ANY = pl.BlockSpec(memory_space=pl.ANY)


def gather_both(x, stat, row_n, col_n):
    depth, width = x.shape
    return pl.pallas_call(
        functools.partial(both_kernel, row_n, col_n),
        out_shape=(jax.ShapeDtypeStruct((depth, width * col_n), x.dtype),
                   jax.ShapeDtypeStruct((depth * row_n, width), x.dtype),
                   jax.ShapeDtypeStruct((8 * col_n, 128), x.dtype)),
        in_specs=[ANY, ANY], out_specs=(ANY, ANY, ANY),
        scratch_shapes=sems(col_n, PIECES) + sems(row_n, PIECES) + sems(col_n, 1) + [pltpu.SemaphoreType.DMA((3,))],
        compiler_params=pltpu.CompilerParams(collective_id=0, has_side_effects=True),
        name="gather_both",
    )(x, stat)


def gather_cols(x, stat, row_n):
    depth, width = x.shape
    return pl.pallas_call(
        functools.partial(cols_kernel, row_n),
        out_shape=(jax.ShapeDtypeStruct((depth * row_n, width), x.dtype),
                   jax.ShapeDtypeStruct((8 * row_n, 128), x.dtype)),
        in_specs=[ANY, ANY], out_specs=(ANY, ANY),
        scratch_shapes=sems(row_n, PIECES) + sems(row_n, 1) + [pltpu.SemaphoreType.DMA((2,))],
        compiler_params=pltpu.CompilerParams(collective_id=1, has_side_effects=True),
        name="gather_cols",
    )(x, stat)


def dot(a, b):
    return jnp.dot(a, b, preferred_element_type=jnp.float32, precision=lax.Precision.HIGH)


def fold(x):
    return jnp.sum(x.reshape(x.shape[0] // 8, 8, x.shape[1] // 128, 128), axis=(0, 2))


def shards(row_n, col_n, matrix):
    x_iter = matrix
    stat = fold(matrix * matrix)
    for step in range(ITERS):
        rows_panel, cols_panel, stats = gather_both(x_iter, stat, row_n, col_n)
        square = dot(rows_panel, cols_panel)
        square_panel, stats = gather_cols(square, fold(stats), row_n)
        cube = dot(rows_panel, square_panel)
        if step == 0:
            factor = jnp.sqrt(matrix.shape[0] * row_n / jnp.sum(stats))
            x_iter = factor * (1.5 * x_iter - (0.5 * factor * factor) * cube)
        else:
            x_iter = 1.5 * x_iter - 0.5 * cube
    return x_iter


def solution(mesh):
    body = functools.partial(shards, mesh.shape["row"], mesh.shape["col"])
    return jax.shard_map(body, mesh=mesh, in_specs=(P("row", "col"),), out_specs=P("row", "col"), check_vma=False)
```

time: 625 us -> 561 us (0.90)
  blocking collectives: 42.2 us -> 0 us
  Pallas kernels: 501 us -> 475 us
    psum x1 -> x0, blocking collectives: 42.2 us -> none  [shards(): lax.psum(jnp.sum(matrix * matrix), ('row', 'col'))]
    pallas_call x2, Pallas kernels: 369 us -> 341 us  [gather_both(): pl.pallas_call(functools.partial(both_kernel, row_n, col_n), out_shape=(j...]
where the time goes in v2:
time: 561 us
  Pallas kernels  475 us (85%)
  matrix products  79.6 us (14%)
    pallas_call x2, Pallas kernels, gather_both(): pl.pallas_call(functools.partial(both_kernel, row_n, col_n), out_shape=(j...  341 us
    pallas_call x2, Pallas kernels, gather_cols(): pl.pallas_call(functools.partial(cols_kernel, row_n), out_shape=(jax.Shap...  135 us
    dot_general x4, matrix products, dot(): jnp.dot(a, b, preferred_element_type=jnp.float32, precision=lax.Precision...  79.6 us

profile of v2, /device:TPU:0, one launch (start us, length us, event | category | flops | bytes accessed | tf_op | source)
XLA Modules:
  0.0 561.1 jit_solution(16663154306033762317)
XLA Ops:
  0.0 2.7 bitcast_reduce_fusion.s_ref
  2.7 171.9 %gather_both.2 = (f32[1024,4096]{1,0:T(8,128)}, f32[4096,512]{1,0:T(8,128)}, f32[64,128]{1,0:T(8,128)}) custom-call(f32[1024,512]{1,0:T(8,128)} %x_ref.1, f32[8,128]{1,0:T(8,128)} %bitcast_reduce_fusion.s_ref), custom_call_target="tpu_custom_call" | custom-call | tf_op jit(solution)/shard_map/gather_both/pallas_call | solution.py:180
  174.6 0.0 copy-start.3
  174.6 0.0 copy-start
  174.6 19.4 %fusion.x_ref = f32[1024,512]{1,0:T(8,128)} fusion(f32[1024,4096]{1,0:T(8,128)} %get-tuple-element.14, f32[4096,512]{1,0:T(8,128)} %get-tuple-element.15), kind=kOutput, calls=%fused_computation.5 | convolution fusion | flops 12884901888 | bytes 27262976 | tf_op jit(solution)/shard_map/dot_general | solution.py:206
  194.1 0.0 copy-done.3
  194.1 0.6 bitcast_reduce_fusion.2.s_ref
  194.7 67.5 %gather_cols.2 = (f32[4096,512]{1,0:T(8,128)}, f32[32,128]{1,0:T(8,128)}) custom-call(f32[1024,512]{1,0:T(8,128)} %fusion.x_ref, f32[8,128]{1,0:T(8,128)} %bitcast_reduce_fusion.2.s_ref), custom_call_target="tpu_custom_call" | custom-call | tf_op jit(solution)/shard_map/gather_cols/pallas_call | solution.py:194
  262.2 1.3 reduce_sum.38
  264.2 0.0 copy-done
  264.3 21.1 %subtract_multiply_fusion.x_ref = f32[1024,512]{1,0:T(8,128)} fusion(f32[1024,512]{1,0:T(8,128)S(1)} %copy-done, f32[1024,4096]{1,0:T(8,128)} %get-tuple-element.14, f32[4096,512]{1,0:T(8,128)} %get-tuple-element.18, f32[]{:T(128)S(6)} %mul.37, f32[]{:T(128)S(6)} %sqrt.3), kind=kOutput, calls=%fused_computation.2 | convolution fusion | flops 12886999040 | bytes 29360136 | tf_op jit(solution)/shard_map/dot_general | solution.py:206
  285.3 168.8 %gather_both.3 = (f32[1024,4096]{1,0:T(8,128)}, f32[4096,512]{1,0:T(8,128)}, f32[64,128]{1,0:T(8,128)}) custom-call(f32[1024,512]{1,0:T(8,128)} %subtract_multiply_fusion.x_ref, f32[8,128]{1,0:T(8,128)} %bitcast_reduce_fusion.s_ref), custom_call_target="tpu_custom_call" | custom-call | tf_op jit(solution)/shard_map/gather_both/pallas_call | solution.py:180
  454.1 0.0 copy-start.2
  454.1 0.0 copy-start.1
  454.1 19.5 %fusion.1.x_ref = f32[1024,512]{1,0:T(8,128)} fusion(f32[1024,4096]{1,0:T(8,128)} %get-tuple-element.19, f32[4096,512]{1,0:T(8,128)} %get-tuple-element.20), kind=kOutput, calls=%fused_computation.6 | convolution fusion | flops 12884901888 | bytes 27262976 | tf_op jit(solution)/shard_map/dot_general | solution.py:206
  473.7 0.0 copy-done.2
  473.7 0.6 bitcast_reduce_fusion.1.s_ref
  474.3 67.3 %gather_cols.3 = (f32[4096,512]{1,0:T(8,128)}, f32[32,128]{1,0:T(8,128)}) custom-call(f32[1024,512]{1,0:T(8,128)} %fusion.1.x_ref, f32[8,128]{1,0:T(8,128)} %bitcast_reduce_fusion.1.s_ref), custom_call_target="tpu_custom_call" | custom-call | tf_op jit(solution)/shard_map/gather_cols/pallas_call | solution.py:194
  541.6 0.0 copy-done.1
  541.6 19.6 %multiply_subtract_fusion = f32[1024,512]{1,0:T(8,128)} fusion(f32[1024,512]{1,0:T(8,128)S(1)} %copy-done.1, f32[1024,4096]{1,0:T(8,128)} %get-tuple-element.19, f32[4096,512]{1,0:T(8,128)} %get-tuple-element.22), kind=kOutput, calls=%fused_computation.1 | convolution fusion | flops 12886474752 | bytes 29360128 | tf_op jit(solution)/shard_map/dot_general | solution.py:206
Async XLA Ops:
  174.6 19.5 %copy-start.3 = (f32[64,128]{1,0:T(8,128)S(1)}, f32[64,128]{1,0:T(8,128)}, u32[]{:S(2)}) copy-start(f32[64,128]{1,0:T(8,128)} %get-tuple-element.16) | copy-start | bytes 98308
  174.6 89.6 %copy-start = (f32[1024,512]{1,0:T(8,128)S(1)}, f32[1024,512]{1,0:T(8,128)}, u32[]{:S(2)}) copy-start(f32[1024,512]{1,0:T(8,128)} %x_ref.1) | copy-start | bytes 6291460
  454.1 19.6 %copy-start.2 = (f32[64,128]{1,0:T(8,128)S(1)}, f32[64,128]{1,0:T(8,128)}, u32[]{:S(2)}) copy-start(f32[64,128]{1,0:T(8,128)} %get-tuple-element.21) | copy-start | bytes 98308
  454.1 87.4 %copy-start.1 = (f32[1024,512]{1,0:T(8,128)S(1)}, f32[1024,512]{1,0:T(8,128)}, u32[]{:S(2)}) copy-start(f32[1024,512]{1,0:T(8,128)} %subtract_multiply_fusion.x_ref) | copy-start | bytes 6291460
